TPU v7x, 32 devices: a whole 2x2x4 slice. The times are simulated.
32 devices in a mesh: ens: 4 (over y, x), zero: 2 (over core), cols: 4 (over z).
Axes of the slice: x: 2, y: 2, z: 4, core: 2. Of those that a mesh axis runs over, the one named last changes fastest.
Arguments:
- one_gate: float32 [8192, 8192], P(('ens', 'zero'), 'cols'), parts along dimension 0, may hold values from -0.1875 to 0.1875
- other_gate: float32 [8192, 8192], P(('ens', 'zero'), 'cols'), parts along dimension 0, may hold values from -0.125 to 0.125
- one_up: float32 [8192, 8192], P(('ens', 'zero'), 'cols'), parts along dimension 0, may hold values from -0.1875 to 0.1875
- other_up: float32 [8192, 8192], P(('ens', 'zero'), 'cols'), parts along dimension 0, may hold values from -0.125 to 0.125
- mix_share: float32 [8192], P(('ens', 'zero')), parts along dimension 0, may hold values from 0.2 to 0.8
- norm_train: float32 [8192], P(('ens', 'zero', 'cols')), parts along dimension 0, may hold values from 0.25 to 1.75
- norm_step: float32 [8192], P(('ens', 'zero', 'cols')), parts along dimension 0, may hold values from -0.3 to 0.3
Outputs:
- serve_gate: bfloat16 [8192, 8192], P('ens', 'cols'), parts along dimension 0
- serve_up: bfloat16 [8192, 8192], P('ens', 'cols'), parts along dimension 0
- factor_gate: float32 [32768], P(('ens', 'cols')), parts along dimension 0
- factor_up: float32 [32768], P(('ens', 'cols')), parts along dimension 0
- serve_norm: bfloat16 [8192], P('ens'), parts along dimension 0
There are 4 independent parts, one for each index of `ens`. A program takes and returns all parts, laid end to end along the dimension named above; each array names one. Nothing has to cross between parts.
All inputs are finite; a program needn't handle non-finite values. Where the computation divides by a largest or mean magnitude, that divisor is 1e-20 or more.
Results may differ from a plain program's by a relative error of at most 0.001.
Values may be sent and summed in bfloat16 or wider, within the bound.
A program may use at most 128 MiB of HBM per device.

v0:
```python
import jax
import jax.numpy as jnp
from jax import lax
from jax.sharding import PartitionSpec as P

D_MODEL = 2048


def local(one_gate, other_gate, one_up, other_up, mix_share, norm_train, norm_step):
    fresh_gate = mix_share[:, None] * one_gate + (1.0 - mix_share[:, None]) * other_gate
    fresh_up = mix_share[:, None] * one_up + (1.0 - mix_share[:, None]) * other_up
    total_gate, total_up = lax.psum(
        (jnp.sum(jnp.abs(fresh_gate), axis=0), jnp.sum(jnp.abs(fresh_up), axis=0)), "zero"
    )
    factor_gate = total_gate / D_MODEL
    factor_up = total_up / D_MODEL
    narrow_gate, narrow_up = (
        (fresh_gate / factor_gate).astype(jnp.bfloat16),
        (fresh_up / factor_up).astype(jnp.bfloat16),
    )
    serve_gate, serve_up = (
        lax.all_gather(narrow_gate, "zero", axis=0, tiled=True),
        lax.all_gather(narrow_up, "zero", axis=0, tiled=True),
    )
    serve_norm = lax.all_gather(
        (norm_train + norm_step).astype(jnp.bfloat16), ("zero", "cols"), axis=0, tiled=True
    )
    return (serve_gate, serve_up, factor_gate, factor_up, serve_norm)


def solution(mesh):
    return jax.shard_map(
        local,
        mesh=mesh,
        in_specs=(
            P(("ens", "zero"), "cols"),
            P(("ens", "zero"), "cols"),
            P(("ens", "zero"), "cols"),
            P(("ens", "zero"), "cols"),
            P(("ens", "zero")),
            P(("ens", "zero", "cols")),
            P(("ens", "zero", "cols")),
        ),
        out_specs=(
            P("ens", "cols"),
            P("ens", "cols"),
            P(("ens", "cols")),
            P(("ens", "cols")),
            P("ens"),
        ),
        check_vma=False,
    )
```

profile of v0, /device:TPU:0, one launch (start us, length us, event | category | flops | bytes accessed | tf_op | source)
XLA Modules:
  0.0 111.0 jit_solution(9187006619748475103)
XLA Ops:
  7.2 0.0 all-gather.4.cloned.1.call-start
  7.2 0.7 broadcast_subtract_fusion
  7.9 0.0 copy-start
  7.9 13.3 %abs_reduce_fusion = (f32[2048]{0:T(1024)S(1)}, f32[2048]{0:T(1024)S(1)}) fusion(f32[1024,2048]{1,0:T(8,128)} %param.10, f32[1024]{0:T(1024)S(1)} %broadcast_subtract_fusion, f32[1024,2048]{1,0:T(8,128)} %param.9, f32[1024]{0:T(1024)} %param.11, f32[1024,2048]{1,0:T(8,128)} %param.8, f32[1024,2048]{1,0:T(8,128)} %param.7), kind=kLoop, calls=%fused_computation.1 | loop fusion | flops 20967424 | bytes 33579008 | tf_op jit(solution)/shard_map/reduce_sum | solution.py:13
  21.2 3.6 %all-reduce = (f32[2048]{0:T(1024)S(1)}, f32[2048]{0:T(1024)S(1)}) all-reduce(f32[2048]{0:T(1024)S(1)} %get-tuple-element.6, f32[2048]{0:T(1024)S(1)} %get-tuple-element.5), channel_id=1, replica_groups=mesh['ens'=4,'zero'=2,'cols'=4] {'zero'}, use_global_device_ids=true, to_apply=%region_1.0 | all-reduce | flops 4096 | bytes 32768 | tf_op jit(solution)/shard_map/psum | solution.py:12
  24.8 0.0 copy-start.1
  24.8 0.0 copy-start.2
  24.8 0.0 copy-done
  24.9 16.8 %divide_convert_fusion = (bf16[1024,2048]{1,0:T(8,128)(2,1)}, bf16[1024,2048]{1,0:T(8,128)(2,1)}) fusion(f32[2048]{0:T(1024)S(1)} %get-tuple-element.21, f32[1024,2048]{1,0:T(8,128)} %param.10, f32[1024]{0:T(1024)S(1)} %broadcast_subtract_fusion, f32[1024,2048]{1,0:T(8,128)} %param.9, f32[1024]{0:T(1024)S(1)} %copy-done, f32[2048]{0:T(1024)S(1)} %get-tuple-element.20, ...), kind=kLoop, calls=%fused_computation | loop fusion | flops 20971520 | bytes 41967616 | tf_op jit(solution)/shard_map/convert_element_type | solution.py:19
  41.6 0.0 copy-done.1
  41.6 0.0 copy-done.2
  41.6 0.0 copy-start.3
  41.7 0.0 copy-start.4
  41.7 0.0 all-gather.4.cloned.1.call-update
  41.7 0.0 all-gather.6.cloned.1.call-start
  41.7 0.7 all-gather.6.cloned.1.call-update
  42.4 0.0 copy-done.3
  42.5 0.0 copy-done.4
  42.5 17.5 %all-gather = bf16[8,1,256]{2,1,0:T(2,128)(2,1)S(1)} all-gather(bf16[1,1,256]{2,1,0:T(2,128)(2,1)S(1)} %reshape.15), channel_id=1, replica_groups=mesh['ens'=4,'zero'=2,'cols'=4] {'zero','cols'}, dimensions={0}, use_global_device_ids=true | all-gather | bytes 4608 | tf_op jit(solution)/shard_map/all_gather | solution.py:25
  60.0 0.6 copy.12
  60.6 3.5 %all-gather.4.cloned.1.call-done = bf16[2048,2048]{1,0:T(8,128)(2,1)} async-done(((bf16[1024,2048]{1,0:T(8,128)(2,1)}), bf16[2048,2048]{1,0:T(8,128)(2,1)}) %all-gather.4.cloned.1.call-update) | async-done | bytes 8388624 | tf_op jit(solution)/shard_map/all_gather | solution.py:22
  64.1 23.2 %all-gather.6.cloned.1.call-done = bf16[2048,2048]{1,0:T(8,128)(2,1)} async-done(((bf16[1024,2048]{1,0:T(8,128)(2,1)}), bf16[2048,2048]{1,0:T(8,128)(2,1)}) %all-gather.6.cloned.1.call-update) | async-done | bytes 8388624 | tf_op jit(solution)/shard_map/all_gather | solution.py:23
  87.3 8.4 %copy.15 = bf16[2048,2048]{1,0:T(8,128)(2,1)} copy(bf16[2048,2048]{1,0:T(8,128)(2,1)} %all-gather.4.cloned.1.call-done) | data formatting | bytes 16777216
  95.7 8.4 %copy.16 = bf16[2048,2048]{1,0:T(8,128)(2,1)} copy(bf16[2048,2048]{1,0:T(8,128)(2,1)} %all-gather.6.cloned.1.call-done) | data formatting | bytes 16777216
  (4 shorter events, 0.0 us)
Async XLA Ops:
  7.2 56.9 %all-gather.4.cloned.1.call-start = ((), (), s32[]{:S(2)}) async-start(), calls=%async_computation | async-start | bytes 12582912 | tf_op jit(solution)/shard_map/all_gather | solution.py:22
  7.9 16.9 %copy-start = (f32[1024]{0:T(1024)S(1)}, f32[1024]{0:T(1024)}, u32[]{:S(2)}) copy-start(f32[1024]{0:T(1024)} %param.11) | copy-start | bytes 12292
  24.8 16.8 %copy-start.1 = (f32[2048]{0:T(1024)}, f32[2048]{0:T(1024)S(1)}, u32[]{:S(2)}) copy-start(f32[2048]{0:T(1024)S(1)} %get-tuple-element.21) | copy-start | bytes 24580
  24.8 16.8 %copy-start.2 = (f32[2048]{0:T(1024)}, f32[2048]{0:T(1024)S(1)}, u32[]{:S(2)}) copy-start(f32[2048]{0:T(1024)S(1)} %get-tuple-element.20) | copy-start | bytes 24580
  41.6 0.8 copy-start.3
  41.7 0.8 copy-start.4
  41.7 45.6 %all-gather.6.cloned.1.call-start = ((), (), s32[]{:S(2)}) async-start(), calls=%async_computation.1 | async-start | bytes 12582912 | tf_op jit(solution)/shard_map/all_gather | solution.py:23
Sparse Core Ops, SparseCore 0:
  41.8 22.2 all-gather.3
  66.2 21.0 all-gather.5
where the time goes:
time: 111 us
  other arithmetic  30.8 us (28%)
  waiting for transfers between devices  27.4 us (25%)
  blocking collectives  21.1 us (19%)
  local copies, waits for them, and re-layouts  17.5 us (16%)
  between operations  14.1 us (13%)
    all_gather x1, waiting for transfers between devices, local(): lax.all_gather(narrow_up, 'zero', axis=0, tiled=True)  23.2 us
    unnamed x14, local copies, waits for them, and re-layouts  17.5 us
    all_gather x1, blocking collectives, local(): lax.all_gather((norm_train + norm_step).astype(jnp.bfloat16), ('zero', 'c...  17.5 us
    convert_element_type x1, other arithmetic, local(): (fresh_up / factor_up).astype(jnp.bfloat16)  16.8 us
    reduce_sum x1, other arithmetic, local(): jnp.sum(jnp.abs(fresh_up), axis=0)  13.3 us
    psum x1, blocking collectives, local(): lax.psum((jnp.sum(jnp.abs(fresh_gate), axis=0), jnp.sum(jnp.abs(fresh_up)...  3.62 us
    all_gather x1, waiting for transfers between devices, local(): lax.all_gather(narrow_gate, 'zero', axis=0, tiled=True)  3.51 us
  transfers between devices with their start and end apart: 2, of which 2 were waited for; matrix products, arithmetic and copies ran while one was open for 1% of the time, Pallas kernels for 0%

commit v1 on v0

v1 whole, which is shorter than its diff:
```python
import functools

import jax
import jax.numpy as jnp
from jax import lax
from jax.experimental import pallas as pl
from jax.experimental.pallas import tpu as pltpu
from jax.sharding import PartitionSpec as P

MESH = pl.DeviceIdType.MESH
LANES = 128
WIDTH = 256
SLOTS = 4
FRESH = 4
LAG = 2
BLOCK = 64


def exchange(
    n, m,
    one_gate, other_gate, one_up, other_up, mix, norm_train, norm_step,
    gate, up, factor_gate, factor_up, norm,
    one_buf, other_buf, fresh, mixed, sums, norm_buf,
    read_sem, sum_send, sum_recv, data_send, data_recv, norm_send, norm_recv,
):
    me, z = lax.axis_index("zero"), lax.axis_index("cols")
    rows, cols = one_gate.shape
    width = one_buf.shape[-1]
    per = cols // width
    base = pl.multiple_of(me * rows, rows)
    block = min(BLOCK, rows)
    work = [
        (src, other, out, factor, k)
        for src, other, out, factor in (
            (one_gate, other_gate, gate, factor_gate),
            (one_up, other_up, up, factor_up),
        )
        for k in range(per)
    ]
    total = len(work)

    def reads(c):
        src, other, _, _, k = work[c]
        at, slot = pl.ds(k * width, width), c % SLOTS
        return (
            pltpu.make_async_copy(src.at[:, at], one_buf.at[slot], read_sem.at[0, slot]),
            pltpu.make_async_copy(other.at[:, at], other_buf.at[slot], read_sem.at[1, slot]),
        )

    def sum_copy(c, d):
        return pltpu.make_async_remote_copy(
            src_ref=sums.at[c, me], dst_ref=sums.at[c, me],
            send_sem=sum_send.at[c], recv_sem=sum_recv.at[c],
            device_id={"zero": lax.rem(me + d, n)}, device_id_type=MESH,
        )

    def data_copy(c, d):
        _, _, out, _, k = work[c]
        at = out.at[pl.ds(base, rows), pl.ds(k * width, width)]
        return pltpu.make_async_remote_copy(
            src_ref=at, dst_ref=at,
            send_sem=data_send.at[c], recv_sem=data_recv.at[c],
            device_id={"zero": lax.rem(me + d, n)}, device_id_type=MESH,
        )

    others = [(dz, dc) for dz in range(n) for dc in range(m) if dz or dc]

    def place(dz, dc):
        return {"zero": lax.rem(me + dz, n), "cols": lax.rem(z + dc, m)}

    def norm_copy(i):
        at = norm_buf.at[me * m + z]
        return pltpu.make_async_remote_copy(
            src_ref=at, dst_ref=at,
            send_sem=norm_send.at[i], recv_sem=norm_recv.at[i],
            device_id=place(*others[i]), device_id_type=MESH,
        )

    def blend(c):
        slot, keep = c % SLOTS, c % FRESH
        for copy in reads(c):
            copy.wait()

        def step(r, acc):
            at = pl.ds(pl.multiple_of(r * block, block), block)
            share = mixed[at, :]
            rest = 1.0 - share
            new = []
            for j in range(width // LANES):
                lanes = pl.ds(j * LANES, LANES)
                value = share * one_buf[slot, at, lanes] + rest * other_buf[slot, at, lanes]
                fresh[keep, at, lanes] = value
                new.append(acc[j] + jnp.sum(jnp.abs(value).reshape(-1, 8, LANES), axis=0))
            return tuple(new)

        zero = jnp.zeros((8, LANES), jnp.float32)
        acc = lax.fori_loop(0, rows // block, step, (zero,) * (width // LANES))
        for j in range(width // LANES):
            sums[c, me, :, pl.ds(j * LANES, LANES)] = jnp.sum(acc[j], axis=0, keepdims=True)
        if c + SLOTS < total:
            for copy in reads(c + SLOTS):
                copy.start()

    def scale(c):
        _, _, out, factor_out, k = work[c]
        keep = c % FRESH
        for d in range(1, n):
            sum_copy(c, d).wait()
        factor = sums[c, 0]
        for i in range(1, n):
            factor = factor + sums[c, i]
        factor = factor / (n * rows)
        factor_out[:, pl.ds(k * width, width)] = factor
        inverse = 1.0 / factor

        def step(r, carry):
            at = pl.multiple_of(r * block, block)
            for j in range(width // LANES):
                value = fresh[keep, pl.ds(at, block), pl.ds(j * LANES, LANES)]
                out[pl.ds(base + at, block), pl.ds(k * width + j * LANES, LANES)] = (
                    value * inverse[:, j * LANES:(j + 1) * LANES]
                ).astype(out.dtype)
            return carry

        lax.fori_loop(0, rows // block, step, 0)
        for d in range(1, n):
            data_copy(c, d).start()

    for c in range(min(SLOTS, total)):
        for copy in reads(c):
            copy.start()
    barrier = pltpu.get_barrier_semaphore()
    for dz, dc in others:
        pl.semaphore_signal(barrier, inc=1, device_id=place(dz, dc), device_id_type=MESH)
    norm_buf[me * m + z] = norm_train[...] + norm_step[...]
    for k in range(rows // LANES):
        row = mix[pl.ds(k, 1), :]
        mixed[pl.ds(k * LANES, LANES), :] = jnp.transpose(jnp.broadcast_to(row, (LANES, LANES)))
    pl.semaphore_wait(barrier, len(others))

    for c in range(total + LAG):
        if c < total:
            blend(c)
            for d in range(1, n):
                sum_copy(c, d).start()
        if c == LAG - 1:
            for i in range(len(others)):
                norm_copy(i).start()
        if c >= LAG:
            scale(c - LAG)
    for i in range(len(others)):
        norm_copy(i).wait()
    norm[...] = norm_buf[...]
    for c in range(total):
        for d in range(1, n):
            data_copy(c, d).wait()


def write(
    pieces, gate, up, factor_gate_in, factor_up_in,
    gate_out, up_out, factor_gate, factor_up, sem,
):
    depth = gate.shape[0] // pieces
    copies = [
        pltpu.make_async_copy(
            src.at[pl.ds(i * depth, depth)], dst.at[pl.ds(i * depth, depth)], sem.at[a, i]
        )
        for a, (src, dst) in enumerate(((gate, gate_out), (up, up_out)))
        for i in range(pieces)
    ]
    for copy in copies:
        copy.start()
    factor_gate[...] = factor_gate_in[...]
    factor_up[...] = factor_up_in[...]
    for copy in copies:
        copy.wait()


def local(n, m, one_gate, other_gate, one_up, other_up, mix_share, norm_train, norm_step):
    rows, cols = one_gate.shape
    (own,) = norm_train.shape
    width = min(WIDTH, cols)
    total = 2 * (cols // width)
    whole = (n * rows, cols)
    hbm = pl.BlockSpec(memory_space=pl.ANY)
    vmem = pl.BlockSpec(memory_space=pltpu.VMEM)
    dma = pltpu.SemaphoreType.DMA
    gate, up, factor_gate, factor_up, norm = pl.pallas_call(
        functools.partial(exchange, n, m),
        out_shape=(
            pltpu.VMEM(whole, jnp.bfloat16),
            pltpu.VMEM(whole, jnp.bfloat16),
            jax.ShapeDtypeStruct((1, cols), jnp.float32),
            jax.ShapeDtypeStruct((1, cols), jnp.float32),
            jax.ShapeDtypeStruct((n * m, 1, own), jnp.float32),
        ),
        in_specs=[hbm] * 4 + [vmem] * 3,
        out_specs=(vmem,) * 5,
        scratch_shapes=[
            pltpu.VMEM((SLOTS, rows, width), jnp.float32),
            pltpu.VMEM((SLOTS, rows, width), jnp.float32),
            pltpu.VMEM((FRESH, rows, width), jnp.float32),
            pltpu.VMEM((rows, LANES), jnp.float32),
            pltpu.VMEM((total, n, 1, width), jnp.float32),
            pltpu.VMEM((n * m, 1, own), jnp.float32),
            dma((2, SLOTS)),
            dma((total,)),
            dma((total,)),
            dma((total,)),
            dma((total,)),
            dma((n * m - 1,)),
            dma((n * m - 1,)),
        ],
        compiler_params=pltpu.CompilerParams(
            collective_id=0, has_side_effects=True, vmem_limit_bytes=36 * 2**20
        ),
        name="exchange",
    )(
        one_gate, other_gate, one_up, other_up,
        mix_share.reshape(-1, LANES), norm_train.reshape(1, -1), norm_step.reshape(1, -1),
    )
    pieces = 8
    serve_gate, serve_up, factor_gate, factor_up = pl.pallas_call(
        functools.partial(write, pieces),
        out_shape=(
            jax.ShapeDtypeStruct(whole, jnp.bfloat16),
            jax.ShapeDtypeStruct(whole, jnp.bfloat16),
            jax.ShapeDtypeStruct((1, cols), jnp.float32),
            jax.ShapeDtypeStruct((1, cols), jnp.float32),
        ),
        in_specs=[vmem] * 4,
        out_specs=(hbm, hbm, vmem, vmem),
        scratch_shapes=[dma((2, pieces))],
        compiler_params=pltpu.CompilerParams(vmem_limit_bytes=2**20),
        name="write",
    )(gate, up, factor_gate, factor_up)
    return (
        serve_gate, serve_up, factor_gate.reshape(-1), factor_up.reshape(-1),
        norm.reshape(-1).astype(jnp.bfloat16),
    )


def solution(mesh):
    return jax.shard_map(
        functools.partial(local, mesh.shape["zero"], mesh.shape["cols"]),
        mesh=mesh,
        in_specs=(P(("ens", "zero"), "cols"),) * 4
        + (P(("ens", "zero")), P(("ens", "zero", "cols")), P(("ens", "zero", "cols"))),
        out_specs=(P("ens", "cols"), P("ens", "cols"), P(("ens", "cols")), P(("ens", "cols")), P("ens")),
        check_vma=False,
    )
```

time: 111 us -> 30.2 us (0.27)
  other arithmetic: 30.8 us -> 0.03 us
  waiting for transfers between devices: 27.4 us -> 0 us
  Pallas kernels: 0 us -> 26.7 us
  blocking collectives: 21.1 us -> 0 us
  local copies, waits for them, and re-layouts: 17.5 us -> 2.63 us
  between operations: 14.1 us -> 0.66 us
    pallas_call x0 -> x2, Pallas kernels: none -> 26.7 us  [the longest x1 20.2 us: local(): pl.pallas_call(functools.partial(exchange, n, m), out_shape=(pltpu.VMEM(w...]
    all_gather x2 -> x0, waiting for transfers between devices: 26.7 us -> none  [the longest x1 23.2 us: local(): lax.all_gather(narrow_up, 'zero', axis=0, tiled=True)]
    all_gather x1 -> x0, blocking collectives: 17.5 us -> none  [local(): lax.all_gather((norm_train + norm_step).astype(jnp.bfloat16), ('zero', 'c...]
    convert_element_type x2 -> x1, other arithmetic: 16.8 us -> 0.03 us  [local(): norm.reshape(-1).astype(jnp.bfloat16)]
    unnamed x14 -> x7, local copies, waits for them, and re-layouts: 17.5 us -> 2.63 us
    reduce_sum x1 -> x0, other arithmetic: 13.3 us -> none  [local(): jnp.sum(jnp.abs(fresh_up), axis=0)]
    psum x1 -> x0, blocking collectives: 3.62 us -> none  [local(): lax.psum((jnp.sum(jnp.abs(fresh_gate), axis=0), jnp.sum(jnp.abs(fresh_up)...]
  transfers between devices with their start and end apart: 2 -> 0, of which waited for: 2 -> 0; matrix products, arithmetic and copies ran while one was open for 1% -> 0% of each run, Pallas kernels for 0% -> 0%
where the time goes in v1:
time: 30.2 us; the launch traced here: 30 us
  Pallas kernels  26.7 us (88%)
  local copies, waits for them, and re-layouts  2.63 us (9%)
  between operations  0.66 us (2%)
    pallas_call x1, Pallas kernels, local(): pl.pallas_call(functools.partial(exchange, n, m), out_shape=(pltpu.VMEM(w...  20.2 us
    pallas_call x1, Pallas kernels, local(): pl.pallas_call(functools.partial(write, pieces), out_shape=(jax.ShapeDtyp...  6.57 us
    unnamed x7, local copies, waits for them, and re-layouts  2.63 us

profile of v1, /device:TPU:0, one launch (start us, length us, event | category | flops | bytes accessed | tf_op | source)
XLA Modules:
  0.0 30.0 jit_solution(15286102884823586037)
XLA Ops:
  0.6 0.0 copy-start
  0.6 0.7 %copy-done = f32[1024]{0:T(1024)S(1)} copy-done((f32[1024]{0:T(1024)S(1)}, f32[1024]{0:T(1024)}, u32[]{:S(2)}) %copy-start) | copy-done | bytes 4120
  1.3 0.0 copy-start.1
  1.3 0.7 %copy-done.1 = f32[256]{0:T(256)S(1)} copy-done((f32[256]{0:T(256)S(1)}, f32[256]{0:T(256)}, u32[]{:S(2)}) %copy-start.1) | copy-done | bytes 1048
  2.0 0.0 copy-start.2
  2.0 0.7 %copy-done.2 = f32[256]{0:T(256)S(1)} copy-done((f32[256]{0:T(256)S(1)}, f32[256]{0:T(256)}, u32[]{:S(2)}) %copy-start.2) | copy-done | bytes 1048
  2.7 20.2 %exchange.1 = (bf16[2048,2048]{1,0:T(8,128)(2,1)S(1)}, bf16[2048,2048]{1,0:T(8,128)(2,1)S(1)}, f32[1,2048]{1,0:T(1,128)S(1)}, f32[1,2048]{1,0:T(1,128)S(1)}, f32[8,1,256]{2,1,0:T(1,128)S(1)}) custom-call(f32[1024,2048]{1,0:T(8,128)} %one_gate.1, f32[1024,2048]{1,0:T(8,128)} %other_gate.1, f32[1024,2048]{1,0:T(8,128)} %one_up.1, f32[1024,2048]{1,0:T(8,128)} %other_up.1, ...), custom_call_target="tpu_custom_call" | custom-call | tf_op jit(solution)/shard_map/exchange/pallas_call | solution.py:188
  22.8 6.6 %write.1 = (bf16[2048,2048]{1,0:T(8,128)(2,1)}, bf16[2048,2048]{1,0:T(8,128)(2,1)}, f32[1,2048]{1,0:T(1,128)}, f32[1,2048]{1,0:T(1,128)}) custom-call(bf16[2048,2048]{1,0:T(8,128)(2,1)S(1)} %get-tuple-element.14.gate, bf16[2048,2048]{1,0:T(8,128)(2,1)S(1)} %get-tuple-element.15.up, f32[1,2048]{1,0:T(1,128)S(1)} %get-tuple-element.16.factor_gate_in, ...), custom_call_target="tpu_custom_call" | custom-call | tf_op jit(solution)/shard_map/write/pallas_call | solution.py:223
  29.4 0.6 %copy.12 = bf16[1,2,8,128]{3,1,2,0:T(2,128)(2,1)} copy(bf16[1,2,8,128]{3,2,1,0:T(8,128)(2,1)S(1)} %bitcast.10) | data formatting | bytes 8192
  (1 shorter events, 0.0 us)
Async XLA Ops:
  0.6 0.7 %copy-start = (f32[1024]{0:T(1024)S(1)}, f32[1024]{0:T(1024)}, u32[]{:S(2)}) copy-start(f32[1024]{0:T(1024)} %param.11) | copy-start | bytes 12292
  1.3 0.7 %copy-start.1 = (f32[256]{0:T(256)S(1)}, f32[256]{0:T(256)}, u32[]{:S(2)}) copy-start(f32[256]{0:T(256)} %param.12) | copy-start | bytes 3076
  2.0 0.7 %copy-start.2 = (f32[256]{0:T(256)S(1)}, f32[256]{0:T(256)}, u32[]{:S(2)}) copy-start(f32[256]{0:T(256)} %param.13) | copy-start | bytes 3076
